TPU v7x, 32 devices: a whole 2x2x4 slice. The times are simulated.
32 devices in a mesh: dp: 4 (over y, x), expert: 8 (over z, core).
Axes of the slice: x: 2, y: 2, z: 4, core: 2. Of those that a mesh axis runs over, the one named last changes fastest.
Arguments:
- tokens: bfloat16 [4096, 2048], P(('dp', 'expert')), may hold values from -6 to 6
- expert_ids: int32 [4096, 2], P(('dp', 'expert')), may hold values from 0 to 7, all different within a row; in each aligned block of 128 rows (0 to 127, 128 to 255, ...) at most 40 rows name the same one
- gate_units: int32 [4096, 2], P(('dp', 'expert')), may hold values from 64 to 1023
- capacity: int32 [8], replicated, may hold values from 512 to 1535
- w_gate: bfloat16 [8, 2048, 1408], P('expert', None, 'dp'), may hold values from -0.125 to 0.125
- w_up: bfloat16 [8, 2048, 1408], P('expert', None, 'dp'), may hold values from -0.125 to 0.125
- w_down: bfloat16 [8, 2048, 1408], P('expert', None, 'dp'), may hold values from -0.15625 to 0.15625
Outputs:
- mixed: bfloat16 [4096, 2048], P(('dp', 'expert'))
Inputs may be any that keep to these rules, and one draw needn't show every extreme that they name: `expert_ids`: each row names two different experts; of one device's 128 rows (aligned blocks) no expert is named more than 40 times.
All inputs are finite; a program needn't handle non-finite values.
Results may differ from a plain program's by a relative error of at most 0.0057.
Values may be sent and summed in bfloat16 or wider, within the bound.
No kernel may reach another device: no remote copies, remote signals or barrier semaphores. Data moves between devices by JAX's collectives and lax.ppermute only.
A program may use at most 128 MiB of HBM per device.

v0:
```python
import jax
import jax.numpy as jnp
from jax import lax
from jax.sharding import PartitionSpec as P


def prefix(shard, axis, combine, identity):
    length, here = (lax.axis_size(axis), lax.axis_index(axis))
    everything = lax.all_gather(shard, axis)
    start = jnp.broadcast_to(jnp.asarray(identity, shard.dtype), shard.shape)

    def step(k, before):
        reached = k < here
        new = combine(before, everything[k])
        return jnp.where(reached, new, before)

    return lax.fori_loop(0, length, step, start)


def expert_rows(rows, gate_w, up_w, down_w):
    gate = jnp.dot(rows, gate_w, preferred_element_type=jnp.float32)
    up = jnp.dot(rows, up_w, preferred_element_type=jnp.float32)
    hidden = (jax.nn.silu(gate) * up).astype(jnp.bfloat16)
    return lax.dot_general(
        hidden, down_w, (((1,), (1,)), ((), ())), preferred_element_type=jnp.float32
    )


def add_counts(earlier, later):
    return earlier + later


def local(tokens, expert_ids, gate_units, capacity, w_gate, w_up, w_down):
    tok_rows = tokens.shape[0]
    width = tokens.shape[1]
    n_experts = capacity.shape[0]
    most = max(2, 5 * tok_rows // (2 * n_experts))
    slots_all = n_experts * most
    flat = expert_ids.reshape(-1)
    onehot = (flat[:, None] == jnp.arange(n_experts, dtype=jnp.int32)[None, :]).astype(jnp.int32)
    local_rank = jnp.sum((jnp.cumsum(onehot, axis=0) - onehot) * onehot, axis=1)
    counts = jnp.sum(onehot, axis=0)
    offsets = prefix(counts, ("dp", "expert"), add_counts, jnp.zeros_like(counts))
    global_slot = jnp.sum(onehot * offsets[None, :], axis=1) + local_rank
    limit = jnp.sum(onehot * capacity[None, :], axis=1)
    kept = global_slot < limit
    weight = jnp.where(kept, gate_units.reshape(-1).astype(jnp.float32) / 1024.0, jnp.float32(0.0))
    send_slot = flat * most + local_rank
    chosen = (send_slot[None, :] == jnp.arange(slots_all, dtype=jnp.int32)[:, None]) & kept[None, :]
    placing = jnp.sum(chosen.reshape(slots_all, tok_rows, 2).astype(jnp.int32), axis=2).astype(
        jnp.bfloat16
    )
    outgoing = jnp.dot(placing, tokens, preferred_element_type=jnp.float32).astype(jnp.bfloat16)
    outgoing = outgoing.reshape(n_experts, most, width)
    arrived = lax.all_to_all(outgoing, "expert", split_axis=0, concat_axis=0, tiled=True).reshape(
        slots_all, width
    )
    produced = expert_rows(
        arrived,
        lax.all_gather(w_gate, "dp", axis=2, tiled=True)[0],
        lax.all_gather(w_up, "dp", axis=2, tiled=True)[0],
        lax.all_gather(w_down, "dp", axis=2, tiled=True)[0],
    )
    answer = produced.astype(jnp.bfloat16).reshape(n_experts, most, width)
    back = lax.all_to_all(answer, "expert", split_axis=0, concat_axis=0, tiled=True).reshape(
        slots_all, width
    )
    picked = back[send_slot].astype(jnp.float32) * weight[:, None]
    mixed = jnp.sum(picked.reshape(tok_rows, 2, width), axis=1)
    return mixed.astype(jnp.bfloat16)


def solution(mesh):
    return jax.shard_map(
        local,
        mesh=mesh,
        in_specs=(
            P(("dp", "expert"), None),
            P(("dp", "expert"), None),
            P(("dp", "expert"), None),
            P(),
            P("expert", None, "dp"),
            P("expert", None, "dp"),
            P("expert", None, "dp"),
        ),
        out_specs=P(("dp", "expert"), None),
        check_vma=False,
    )
```

profile of v0, /device:TPU:0, one launch (start us, length us, event | category | flops | bytes accessed | tf_op | source)
XLA Modules:
  0.0 275.7 jit_solution(2728513415111079550)
XLA Ops:
  6.5 0.0 copy-start
  6.5 0.0 all-gather.5.cloned.1.call-start
  6.5 0.7 all-gather.5.cloned.1.call-update
  7.3 0.0 copy-start.1
  7.3 0.0 copy-start.3
  7.3 0.0 copy-start.2
  7.3 0.0 all-gather.7.cloned.1.call-start
  7.3 0.7 all-gather.7.cloned.1.call-update
  8.0 0.0 all-gather.9.cloned.1.call-start
  8.1 0.7 all-gather.9.cloned.1.call-update
  8.8 0.0 copy-done.1
  8.8 0.1 copy.23
  8.9 0.1 eq.39
  9.1 0.1 eq.43
  9.2 0.1 convert_reduce_fusion.1
  9.3 0.2 dynamic-update-slice
  9.6 42.6 %all-reduce = s32[256]{0:T(256)S(1)} all-reduce(s32[256]{0:T(256)S(1)} %dynamic-update-slice), channel_id=2, replica_groups=mesh['dp'=4,'expert'=8] {'dp','expert'}, use_global_device_ids=true, to_apply=%add | all-reduce | flops 256 | bytes 2048
  52.1 0.1 reshape.134
  52.2 0.6 reduce-window.6
  52.8 0.2 slice_reduce_fusion
  53.1 1.3 while.14
  54.4 0.0 copy-done.3
  54.4 0.1 select_reduce_fusion.1
  54.5 0.1 reduce_sum.63
  54.6 0.1 copy.28
  54.7 0.2 reduce_sum.66
  54.8 0.1 copy.27
  54.9 0.2 reduce_sum.68
  55.1 0.1 copy.29
  55.2 0.1 copy.26
  55.2 0.0 copy-done.2
  55.3 0.0 copy-done
  55.3 0.5 convolution_convert_fusion
  55.8 35.6 %all_to_all.10 = bf16[8,40,2048]{2,1,0:T(8,128)(2,1)S(1)} all-to-all(bf16[8,40,2048]{2,1,0:T(8,128)(2,1)S(1)} %bitcast.35), channel_id=1, replica_groups=mesh['dp'=4,'expert'=8] {'expert'}, dimensions={0} | all-to-all | bytes 2621440 | tf_op jit(solution)/shard_map/all_to_all | solution.py:55
  91.4 0.0 all-gather.5.cloned.1.call-done
  91.4 6.1 %fusion.4 = f32[320,1408]{1,0:T(8,128)} fusion(bf16[320,2048]{1,0:T(8,128)(2,1)S(1)} %bitcast.36, bf16[1,2048,1408]{1,2,0:T(8,128)(2,1)} %all-gather.5.cloned.1.call-done), kind=kOutput, calls=%fused_computation.7 | convolution fusion | flops 1845493760 | bytes 8880128 | tf_op jit(solution)/shard_map/dot_general | solution.py:21
  97.5 48.3 %all-gather.7.cloned.1.call-done = bf16[1,2048,1408]{1,2,0:T(8,128)(2,1)} async-done(((bf16[1,2048,352]{1,2,0:T(8,128)(2,1)}), bf16[1,2048,1408]{1,2,0:T(8,128)(2,1)}) %all-gather.7.cloned.1.call-update) | async-done | bytes 5767184 | tf_op jit(solution)/shard_map/all_gather | solution.py:61
  145.8 67.5 %all-gather.9.cloned.1.call-done = bf16[1,2048,1408]{1,2,0:T(8,128)(2,1)} async-done(((bf16[1,2048,352]{1,2,0:T(8,128)(2,1)}), bf16[1,2048,1408]{1,2,0:T(8,128)(2,1)}) %all-gather.9.cloned.1.call-update) | async-done | bytes 5767184 | tf_op jit(solution)/shard_map/all_gather | solution.py:62
  213.4 10.3 %fusion.9 = bf16[320,2048]{1,0:T(8,128)(2,1)} fusion(bf16[1,2048,1408]{1,2,0:T(8,128)(2,1)} %all-gather.9.cloned.1.call-done, bf16[320,2048]{1,0:T(8,128)(2,1)S(1)} %bitcast.37, bf16[1,2048,1408]{1,2,0:T(8,128)(2,1)} %all-gather.7.cloned.1.call-done, f32[320,1408]{1,0:T(8,128)} %fusion.4), kind=kOutput, calls=%fused_computation.10 | convolution fusion | flops 3694346240 | bytes 15958016 | tf_op jit(solution)/shard_map/dot_general | solution.py:24
  223.7 4.6 %all-to-all-start.1 = ((bf16[8,40,2048]{2,1,0:T(8,128)(2,1)}), bf16[8,40,2048]{2,1,0:T(8,128)(2,1)S(1)}, u32[]{:S(2)}, u32[]{:S(2)}) async-start(bf16[8,40,2048]{2,1,0:T(8,128)(2,1)} %bitcast.7), calls=%async_computation.1 | async-start | bytes 2621440 | tf_op jit(solution)/shard_map/all_to_all | solution.py:65
  228.3 0.1 mul.68
  228.4 0.1 copy.30
  228.5 31.9 %all-to-all-done.1 = bf16[8,40,2048]{2,1,0:T(8,128)(2,1)S(1)} async-done(((bf16[8,40,2048]{2,1,0:T(8,128)(2,1)}), bf16[8,40,2048]{2,1,0:T(8,128)(2,1)S(1)}, u32[]{:S(2)}, u32[]{:S(2)}) %all-to-all-start.1) | async-done | bytes 1310752 | tf_op jit(solution)/shard_map/all_to_all | solution.py:65
  260.5 2.3 gather_fusion
  262.8 2.4 reshape.125
  265.2 4.0 %multiply_reduce_fusion = bf16[128,2048]{1,0:T(8,128)(2,1)} fusion(f32[128,2,2048]{2,1,0:T(2,128)S(1)} %reshape.125, f32[128,2]{1,0:T(8,128)S(1)} %copy.30), kind=kLoop, calls=%fused_computation.13 | loop fusion | flops 786432 | bytes 2622464 | tf_op jit(solution)/shard_map/reduce_sum | solution.py:69
  (42 shorter events, 0.7 us)
Async XLA Ops:
  6.5 48.8 %copy-start = (bf16[128,2048]{1,0:T(8,128)(2,1)S(1)}, bf16[128,2048]{1,0:T(8,128)(2,1)}, u32[]{:S(2)}) copy-start(bf16[128,2048]{1,0:T(8,128)(2,1)} %param.9) | copy-start | bytes 1572868
  6.5 84.9 %all-gather.5.cloned.1.call-start = ((), (), s32[]{:S(2)}) async-start(), calls=%async_computation.2 | async-start | bytes 7208960 | tf_op jit(solution)/shard_map/all_gather | solution.py:60
  7.3 1.5 copy-start.1
  7.3 47.1 %copy-start.3 = (s32[8]{0:T(128)S(1)}, s32[8]{0:T(128)}, u32[]{:S(2)}) copy-start(s32[8]{0:T(128)} %param.12) | copy-start | bytes 100
  7.3 47.9 %copy-start.2 = (s32[128,2]{0,1:T(2,128)S(1)}, s32[128,2]{0,1:T(2,128)}, u32[]{:S(2)}) copy-start(s32[128,2]{0,1:T(2,128)} %param.11) | copy-start | bytes 3076
  7.3 138.6 %all-gather.7.cloned.1.call-start = ((), (), s32[]{:S(2)}) async-start(), calls=%async_computation.3 | async-start | bytes 7208960 | tf_op jit(solution)/shard_map/all_gather | solution.py:61
  8.0 205.4 %all-gather.9.cloned.1.call-start = ((), (), s32[]{:S(2)}) async-start(), calls=%async_computation.4 | async-start | bytes 7208960 | tf_op jit(solution)/shard_map/all_gather | solution.py:62
  223.7 36.8 %all-to-all-start.1 = ((bf16[8,40,2048]{2,1,0:T(8,128)(2,1)}), bf16[8,40,2048]{2,1,0:T(8,128)(2,1)S(1)}, u32[]{:S(2)}, u32[]{:S(2)}) async-start(bf16[8,40,2048]{2,1,0:T(8,128)(2,1)} %bitcast.7), calls=%async_computation.1 | async-start | bytes 2621440 | tf_op jit(solution)/shard_map/all_to_all | solution.py:65
Sparse Core Ops, SparseCore 0:
  9.2 69.0 all-gather.4
  80.1 65.6 all-gather.6
  147.7 65.6 all-gather.8
where the time goes:
time: 276 us
  waiting for transfers between devices  150 us (54%)
  blocking collectives  78.1 us (28%)
  matrix products  16.9 us (6%)
  between operations  13.3 us (5%)
  local copies, waits for them, and re-layouts  6.6 us (2%)
  other arithmetic  5.55 us (2%)
  starting transfers between devices  4.68 us (2%)
    all_gather x1, waiting for transfers between devices, local(): lax.all_gather(w_down, 'dp', axis=2, tiled=True)[0]  67.5 us
    all_gather x1, waiting for transfers between devices, local(): lax.all_gather(w_up, 'dp', axis=2, tiled=True)[0]  48.3 us
    unnamed x1, blocking collectives  42.6 us
    all_to_all x1, blocking collectives, local(): lax.all_to_all(outgoing, 'expert', split_axis=0, concat_axis=0, tiled=True)  35.6 us
    all_to_all x1, waiting for transfers between devices, local(): lax.all_to_all(answer, 'expert', split_axis=0, concat_axis=0, tiled=True)  31.9 us
    dot_general x1, matrix products, expert_rows(): lax.dot_general(hidden, down_w, (((1,), (1,)), ((), ())), preferred_eleme...  10.3 us
    dot_general x1, matrix products, expert_rows(): gate = jnp.dot(rows, gate_w, preferred_element_type=jnp.float32)  6.11 us
  transfers between devices with their start and end apart: 4, of which 3 were waited for; matrix products, arithmetic and copies ran while one was open for 4% of the time, Pallas kernels for 0%

commit v1 on v0

--- a/solution.py
+++ b/solution.py
@@ -1,7 +1,42 @@
+import functools
 import jax
 import jax.numpy as jnp
 from jax import lax
 from jax.sharding import PartitionSpec as P
+
+
+def process_task(point, row_dim, t0):
+    w1, work_now = (point.shape[:row_dim], point.shape[row_dim + 1 :])
+    piece_now = jnp.moveaxis(point.reshape(*w1, t0, -1, *work_now), row_dim, 0)
+    return piece_now
+
+
+def trace_the_ticks(values, d_out):
+    values = jnp.moveaxis(values, 0, d_out)
+    a_now = values.shape
+    spare = values.reshape(*a_now[:d_out], a_now[d_out] * a_now[d_out + 1], *a_now[d_out + 2 :])
+    return spare
+
+
+def _fill_fields(sheet, row_axis, state, original):
+    right_arr, main = (lax.axis_size(row_axis), lax.axis_index(row_axis))
+    y_new = process_task(sheet, state, right_arr)
+    ledger = [y_new[main]]
+    b = 1
+    while b < right_arr:
+        carry_in = y_new[(main + b) % right_arr]
+        ledger.append(
+            lax.ppermute(
+                carry_in, row_axis, perm=[(jj, (jj + b) % right_arr) for jj in range(right_arr)]
+            )
+        )
+        b = b + 1
+    y_new = jnp.stack(ledger, 0)[(main - jnp.arange(right_arr)) % right_arr]
+    e_now = trace_the_ticks(y_new, original)
+    return e_now
+
+
+_deliver_targets = functools.partial(_fill_fields, row_axis="expert", state=0, original=0)
 
 
 def prefix(shard, axis, combine, identity):
@@ -62,9 +97,7 @@
         lax.all_gather(w_down, "dp", axis=2, tiled=True)[0],
     )
     answer = produced.astype(jnp.bfloat16).reshape(n_experts, most, width)
-    back = lax.all_to_all(answer, "expert", split_axis=0, concat_axis=0, tiled=True).reshape(
-        slots_all, width
-    )
+    back = _deliver_targets(answer).reshape(slots_all, width)
     picked = back[send_slot].astype(jnp.float32) * weight[:, None]
     mixed = jnp.sum(picked.reshape(tok_rows, 2, width), axis=1)
     return mixed.astype(jnp.bfloat16)

time: 276 us -> 270 us (0.978)
  the two profiles are of different devices: /device:TPU:0 before, /device:TPU:9 now
where the time goes in v1:
time: 270 us
  waiting for transfers between devices  172 us (64%)
  blocking collectives  41.2 us (15%)
  matrix products  17.3 us (6%)
  between operations  13.4 us (5%)
  starting transfers between devices  11.8 us (4%)
  local copies, waits for them, and re-layouts  8.23 us (3%)
  other arithmetic  5.46 us (2%)
    all_gather x1, waiting for transfers between devices, local(): lax.all_gather(w_down, 'dp', axis=2, tiled=True)[0]  67.5 us
    all_gather x1, waiting for transfers between devices, local(): lax.all_gather(w_up, 'dp', axis=2, tiled=True)[0]  49.2 us
    unnamed x1, blocking collectives  41.2 us
    all_to_all x1, waiting for transfers between devices, local(): lax.all_to_all(outgoing, 'expert', split_axis=0, concat_axis=0, tiled=True)  28.5 us
    ppermute x7, waiting for transfers between devices, _fill_fields(): lax.ppermute(carry_in, row_axis, perm=[(jj, (jj + b) % right_arr) for jj...  24.6 us
    dot_general x1, matrix products, expert_rows(): lax.dot_general(hidden, down_w, (((1,), (1,)), ((), ())), preferred_eleme...  9.19 us
    ppermute x7, starting transfers between devices, _fill_fields(): lax.ppermute(carry_in, row_axis, perm=[(jj, (jj + b) % right_arr) for jj...  7.52 us
    dot_general x1, matrix products, expert_rows(): gate = jnp.dot(rows, gate_w, preferred_element_type=jnp.float32)  6.5 us
  transfers between devices with their start and end apart: 11, of which 8 were waited for; matrix products, arithmetic and copies ran while one was open for 4% of the time, Pallas kernels for 0%

profile of v1, /device:TPU:9, one launch (start us, length us, event | category | flops | bytes accessed | tf_op | source)
XLA Modules:
  0.0 270.0 jit_solution(2825350137911415098)
XLA Ops:
  6.5 0.7 all-gather.5.cloned.1.call-update
  7.3 0.0 all-gather.7.cloned.1.call-start
  7.3 0.7 all-gather.7.cloned.1.call-update
  8.0 0.0 all-gather.9.cloned.1.call-start
  8.1 0.7 all-gather.9.cloned.1.call-update
  8.8 0.1 copy.23
  8.9 0.1 eq.49
  9.1 0.1 eq.53
  9.2 0.1 convert_reduce_fusion.1
  9.3 0.2 dynamic-update-slice
  9.6 41.2 %all-reduce = s32[256]{0:T(256)S(1)} all-reduce(s32[256]{0:T(256)S(1)} %dynamic-update-slice), channel_id=2, replica_groups=mesh['dp'=4,'expert'=8] {'dp','expert'}, use_global_device_ids=true, to_apply=%add | all-reduce | flops 256 | bytes 2048
  50.8 0.1 reshape.185
  50.9 0.6 reduce-window.6
  51.5 0.2 slice_reduce_fusion
  51.7 1.3 while.14
  53.0 0.1 select_reduce_fusion.1
  53.1 0.1 reduce_sum.63
  53.3 0.1 copy.28
  53.3 0.2 reduce_sum.66
  53.5 0.1 copy.27
  53.5 0.2 reduce_sum.68
  53.7 0.1 copy.29
  53.8 0.1 copy.26
  54.0 1.6 convolution_convert_fusion
  55.5 4.2 %all-to-all-start = ((bf16[8,40,2048]{2,1,0:T(8,128)(2,1)}), bf16[8,40,2048]{2,1,0:T(8,128)(2,1)S(1)}, u32[]{:S(2)}, u32[]{:S(2)}) async-start(bf16[8,40,2048]{2,1,0:T(8,128)(2,1)} %bitcast.2), calls=%async_computation | async-start | bytes 2621440 | tf_op jit(solution)/shard_map/all_to_all | solution.py:90
  59.8 0.1 mul.68
  60.0 28.5 %all-to-all-done = bf16[8,40,2048]{2,1,0:T(8,128)(2,1)S(1)} async-done(((bf16[8,40,2048]{2,1,0:T(8,128)(2,1)}), bf16[8,40,2048]{2,1,0:T(8,128)(2,1)S(1)}, u32[]{:S(2)}, u32[]{:S(2)}) %all-to-all-start) | async-done | bytes 1310752 | tf_op jit(solution)/shard_map/all_to_all | solution.py:90
  88.4 6.5 %fusion.4 = f32[320,1408]{1,0:T(8,128)} fusion(bf16[320,2048]{1,0:T(8,128)(2,1)S(1)} %bitcast.67, bf16[1,2048,1408]{1,2,0:T(8,128)(2,1)} %all-gather.5.cloned.1.call-done), kind=kOutput, calls=%fused_computation.8 | convolution fusion | flops 1845493760 | bytes 8880128 | tf_op jit(solution)/shard_map/dot_general | solution.py:56
  94.9 49.2 %all-gather.7.cloned.1.call-done = bf16[1,2048,1408]{1,2,0:T(8,128)(2,1)} async-done(((bf16[1,2048,352]{1,2,0:T(8,128)(2,1)}), bf16[1,2048,1408]{1,2,0:T(8,128)(2,1)}) %all-gather.7.cloned.1.call-update) | async-done | bytes 5767184 | tf_op jit(solution)/shard_map/all_gather | solution.py:96
  144.1 67.5 %all-gather.9.cloned.1.call-done = bf16[1,2048,1408]{1,2,0:T(8,128)(2,1)} async-done(((bf16[1,2048,352]{1,2,0:T(8,128)(2,1)}), bf16[1,2048,1408]{1,2,0:T(8,128)(2,1)}) %all-gather.9.cloned.1.call-update) | async-done | bytes 5767184 | tf_op jit(solution)/shard_map/all_gather | solution.py:97
  211.7 9.2 %fusion.9 = bf16[320,2048]{1,0:T(8,128)(2,1)S(1)} fusion(bf16[1,2048,1408]{1,2,0:T(8,128)(2,1)} %all-gather.9.cloned.1.call-done, bf16[320,2048]{1,0:T(8,128)(2,1)S(1)} %bitcast.68, bf16[1,2048,1408]{1,2,0:T(8,128)(2,1)} %all-gather.7.cloned.1.call-done, f32[320,1408]{1,0:T(8,128)} %fusion.4), kind=kOutput, calls=%fused_computation.11 | convolution fusion | flops 3694346240 | bytes 15958016 | tf_op jit(solution)/shard_map/dot_general | solution.py:59
  220.9 0.9 dynamic-slice_bitcast_fusion
  221.8 1.9 collective-permute-start
  223.7 0.1 copy.30
  223.8 1.3 collective-permute-start.1
  225.1 0.2 collective-permute-start.2
  225.3 1.2 collective-permute-start.3
  226.5 1.7 collective-permute-start.4
  228.3 1.2 collective-permute-start.5
  229.4 2.0 collective-permute-done.1
  231.4 16.9 %collective-permute-done.2 = bf16[1,40,2048]{2,1,0:T(8,128)(2,1)S(1)} collective-permute-done((bf16[1,40,2048]{2,1,0:T(8,128)(2,1)}, bf16[1,40,2048]{2,1,0:T(8,128)(2,1)S(1)}, u32[]{:S(2)}, u32[]{:S(2)}) %collective-permute-start.2) | collective-permute-done | bytes 163872 | tf_op jit(solution)/shard_map/ppermute | solution.py:29
  248.4 3.5 %collective-permute-done.3 = bf16[1,40,2048]{2,1,0:T(8,128)(2,1)S(1)} collective-permute-done((bf16[1,40,2048]{2,1,0:T(8,128)(2,1)}, bf16[1,40,2048]{2,1,0:T(8,128)(2,1)S(1)}, u32[]{:S(2)}, u32[]{:S(2)}) %collective-permute-start.3) | collective-permute-done | bytes 163872 | tf_op jit(solution)/shard_map/ppermute | solution.py:29
  251.9 2.1 collective-permute-done.5
  254.0 0.1 collective-permute-done.6
  254.1 0.6 gather_fusion
  254.8 2.3 gather_fusion.1
  257.1 2.4 reshape.166
  259.5 3.9 %multiply_reduce_fusion = bf16[128,2048]{1,0:T(8,128)(2,1)} fusion(f32[128,2,2048]{2,1,0:T(2,128)S(1)} %reshape.166, f32[128,2]{1,0:T(8,128)S(1)} %copy.30), kind=kLoop, calls=%fused_computation.14 | loop fusion | flops 786432 | bytes 2622464 | tf_op jit(solution)/shard_map/reduce_sum | solution.py:102
  (64 shorter events, 0.9 us)
Async XLA Ops:
  6.5 47.4 %copy-start = (bf16[128,2048]{1,0:T(8,128)(2,1)S(1)}, bf16[128,2048]{1,0:T(8,128)(2,1)}, u32[]{:S(2)}) copy-start(bf16[128,2048]{1,0:T(8,128)(2,1)} %param.9) | copy-start | bytes 1572868
  6.5 81.9 %all-gather.5.cloned.1.call-start = ((), (), s32[]{:S(2)}) async-start(), calls=%async_computation.1 | async-start | bytes 7208960 | tf_op jit(solution)/shard_map/all_gather | solution.py:95
  7.3 1.5 copy-start.1
  7.3 45.8 %copy-start.3 = (s32[8]{0:T(128)S(1)}, s32[8]{0:T(128)}, u32[]{:S(2)}) copy-start(s32[8]{0:T(128)} %param.12) | copy-start | bytes 100
  7.3 136.8 %all-gather.7.cloned.1.call-start = ((), (), s32[]{:S(2)}) async-start(), calls=%async_computation.2 | async-start | bytes 7208960 | tf_op jit(solution)/shard_map/all_gather | solution.py:96
  8.0 45.8 %copy-start.2 = (s32[128,2]{0,1:T(2,128)S(1)}, s32[128,2]{0,1:T(2,128)}, u32[]{:S(2)}) copy-start(s32[128,2]{0,1:T(2,128)} %param.11) | copy-start | bytes 3076
  8.0 203.6 %all-gather.9.cloned.1.call-start = ((), (), s32[]{:S(2)}) async-start(), calls=%async_computation.3 | async-start | bytes 7208960 | tf_op jit(solution)/shard_map/all_gather | solution.py:97
  55.5 32.9 %all-to-all-start = ((bf16[8,40,2048]{2,1,0:T(8,128)(2,1)}), bf16[8,40,2048]{2,1,0:T(8,128)(2,1)S(1)}, u32[]{:S(2)}, u32[]{:S(2)}) async-start(bf16[8,40,2048]{2,1,0:T(8,128)(2,1)} %bitcast.2), calls=%async_computation | async-start | bytes 2621440 | tf_op jit(solution)/shard_map/all_to_all | solution.py:90
  221.8 6.5 %collective-permute-start = (bf16[1,40,2048]{2,1,0:T(8,128)(2,1)}, bf16[1,40,2048]{2,1,0:T(8,128)(2,1)S(1)}, u32[]{:S(2)}, u32[]{:S(2)}) collective-permute-start(bf16[1,40,2048]{2,1,0:T(8,128)(2,1)} %get-tuple-element.119), channel_id=1, source_target_pairs={{0,1},{1,2},{2,3},{3,4},{4,5},{5,6},{6,7},{7,0},{8,9},{9,10},{10,1... | collective-permute-start | bytes 491528 | tf_op jit(solution)/shard_map/ppermute | solution.py:29
  223.8 7.6 %collective-permute-start.1 = (bf16[1,40,2048]{2,1,0:T(8,128)(2,1)}, bf16[1,40,2048]{2,1,0:T(8,128)(2,1)S(1)}, u32[]{:S(2)}, u32[]{:S(2)}) collective-permute-start(bf16[1,40,2048]{2,1,0:T(8,128)(2,1)} %get-tuple-element.118), channel_id=1, source_target_pairs={{0,2},{1,3},{2,4},{3,5},{4,6},{5,7},{6,0},{7,1},{8,10},{9,11},{10,... | collective-permute-start | bytes 491528 | tf_op jit(solution)/shard_map/ppermute | solution.py:29
  225.1 23.3 %collective-permute-start.2 = (bf16[1,40,2048]{2,1,0:T(8,128)(2,1)}, bf16[1,40,2048]{2,1,0:T(8,128)(2,1)S(1)}, u32[]{:S(2)}, u32[]{:S(2)}) collective-permute-start(bf16[1,40,2048]{2,1,0:T(8,128)(2,1)} %get-tuple-element.117), channel_id=1, source_target_pairs={{0,3},{1,4},{2,5},{3,6},{4,7},{5,0},{6,1},{7,2},{8,11},{9,12},{10,... | collective-permute-start | bytes 491528 | tf_op jit(solution)/shard_map/ppermute | solution.py:29
  225.3 26.5 %collective-permute-start.3 = (bf16[1,40,2048]{2,1,0:T(8,128)(2,1)}, bf16[1,40,2048]{2,1,0:T(8,128)(2,1)S(1)}, u32[]{:S(2)}, u32[]{:S(2)}) collective-permute-start(bf16[1,40,2048]{2,1,0:T(8,128)(2,1)} %get-tuple-element.116), channel_id=1, source_target_pairs={{0,4},{1,5},{2,6},{3,7},{4,0},{5,1},{6,2},{7,3},{8,12},{9,13},{10,... | collective-permute-start | bytes 491528 | tf_op jit(solution)/shard_map/ppermute | solution.py:29
  226.5 25.3 %collective-permute-start.4 = (bf16[1,40,2048]{2,1,0:T(8,128)(2,1)}, bf16[1,40,2048]{2,1,0:T(8,128)(2,1)S(1)}, u32[]{:S(2)}, u32[]{:S(2)}) collective-permute-start(bf16[1,40,2048]{2,1,0:T(8,128)(2,1)} %get-tuple-element.115), channel_id=1, source_target_pairs={{0,5},{1,6},{2,7},{3,0},{4,1},{5,2},{6,3},{7,4},{8,13},{9,14},{10,... | collective-permute-start | bytes 491528 | tf_op jit(solution)/shard_map/ppermute | solution.py:29
  228.3 25.8 %collective-permute-start.5 = (bf16[1,40,2048]{2,1,0:T(8,128)(2,1)S(1)}, bf16[1,40,2048]{2,1,0:T(8,128)(2,1)S(1)}, u32[]{:S(2)}, u32[]{:S(2)}) collective-permute-start(bf16[1,40,2048]{2,1,0:T(8,128)(2,1)S(1)} %get-tuple-element.114), channel_id=1, source_target_pairs={{0,6},{1,7},{2,0},{3,1},{4,2},{5,3},{6,4},{7,5},{8,14},{9,15},{10,... | collective-permute-start | bytes 491528 | tf_op jit(solution)/shard_map/ppermute | solution.py:29
  231.4 22.7 %collective-permute-start.6 = (bf16[1,40,2048]{2,1,0:T(8,128)(2,1)S(1)}, bf16[1,40,2048]{2,1,0:T(8,128)(2,1)S(1)}, u32[]{:S(2)}, u32[]{:S(2)}) collective-permute-start(bf16[1,40,2048]{2,1,0:T(8,128)(2,1)S(1)} %get-tuple-element.113), channel_id=1, source_target_pairs={{0,7},{1,0},{2,1},{3,2},{4,3},{5,4},{6,5},{7,6},{8,15},{9,8},{10,9... | collective-permute-start | bytes 491528 | tf_op jit(solution)/shard_map/ppermute | solution.py:29
Sparse Core Ops, SparseCore 0:
  9.2 67.3 all-gather.4
  78.4 65.6 all-gather.6
  146.0 65.6 all-gather.8
